TPU v7x, 32 devices: a whole 2x2x4 slice. The times are simulated.
32 devices in a mesh: clip: 2 (over y), seq: 4 (over z), head: 4 (over x, core).
Axes of the slice: x: 2, y: 2, z: 4, core: 2. Of those that a mesh axis runs over, the one named last changes fastest.
Arguments:
- queries: bfloat16 [16, 4, 16, 3072], P(('clip', 'head'), 'seq'), parts along dimension 0, may hold values from -15 to 15
- attn_keys: bfloat16 [16, 4, 16, 3072], P(('clip', 'head'), 'seq'), parts along dimension 0, may hold values from -5 to 5
- attn_values: bfloat16 [16, 4, 16, 3072], P(('clip', 'head'), 'seq'), parts along dimension 0, may hold values from -5 to 5
- residual: bfloat16 [16, 4, 16, 5120], P(('clip', 'head'), 'seq'), parts along dimension 0, may hold values from -6 to 6
- out_weight: bfloat16 [3072, 5120], P('head', 'seq'), may hold values from -0.109375 to 0.109375
- out_gate: float32 [5120], replicated, may hold values from 0.3 to 3
- head_shift: float32 [5120], replicated, may hold values from -3 to 3
- head_scale: float32 [5120], replicated, may hold values from -1.5 to 1.5
- head_weight: bfloat16 [5120, 64], replicated, may hold values from -0.078125 to 0.078125
- head_bias: float32 [64], replicated, may hold values from -3 to 3
- conv_weight: bfloat16 [3, 3, 3, 16, 384], replicated, may hold values from -0.3125 to 0.3125
- conv_bias: float32 [384], replicated, may hold values from -3 to 3
- norm_gain: float32 [384], replicated, may hold values from 0.5 to 2
Outputs:
- hidden: bfloat16 [16, 4, 16, 5120], P(('clip', 'head'), 'seq'), parts along dimension 0
- features: bfloat16 [16, 8, 32, 384], P(('clip', 'head'), 'seq'), parts along dimension 0
There are 2 independent parts, one for each index of `clip`. A program takes and returns all parts, laid end to end along the dimension named above; an argument that names none is the same for every part. Nothing has to cross between parts.
All inputs are finite; a program needn't handle non-finite values.
Results may differ from a plain program's by a relative error of at most 0.013.
Values may be sent and summed in bfloat16 or wider, within the bound.
No kernel may reach another device: no remote copies, remote signals or barrier semaphores. Data moves between devices by JAX's collectives and lax.ppermute only.
A program may use at most 128 MiB of HBM per device.

v0:
```python
import jax
import jax.numpy as jnp
from jax import lax
from jax.sharding import PartitionSpec as P

HEAD_DIM = 128


def from_behind(value, axis, steps):
    count = lax.axis_size(axis)
    first, last = (max(0, -steps), min(count, count - steps))
    return lax.ppermute(value, axis, [(source, source + steps) for source in range(first, last)])


def padded_2(x, sides, width):
    for axis, dim in sides:
        peers, length = (lax.axis_size(axis), x.shape[dim])
        up = [(i, (i + 1) % peers) for i in range(peers - 1)]
        down = [(j, i) for i, j in up]
        last = lax.slice_in_dim(x, length - width, length, axis=dim)
        first = lax.slice_in_dim(x, 0, width, axis=dim)
        before = lax.ppermute(last, axis, up)
        after = lax.ppermute(first, axis, down)
        x = jnp.concatenate([before, x, after], axis=dim)
    return x


def head_latent(hidden, head_shift, head_scale, head_weight, head_bias):
    values = hidden.astype(jnp.float32)
    center = values - jnp.mean(values, -1, keepdims=True)
    spread = jnp.mean(center * center, -1, keepdims=True)
    normed = (center * lax.rsqrt(spread + 1e-06) * (1.0 + head_scale) + head_shift).astype(
        jnp.bfloat16
    )
    flat = normed.reshape(-1, normed.shape[-1])
    latent = (jnp.dot(flat, head_weight, preferred_element_type=jnp.float32) + head_bias).astype(
        jnp.bfloat16
    )
    frames, height, breadth = (hidden.shape[0], hidden.shape[1], hidden.shape[2])
    channels = head_weight.shape[1] // 4
    patches = latent.reshape(frames, height, breadth, 2, 2, channels).transpose(0, 1, 3, 2, 4, 5)
    return patches.reshape(frames, height * 2, breadth * 2, channels)


def convolve(padded, frames, conv_weight, conv_bias, norm_gain):
    height = padded.shape[1] - 2
    breadth = padded.shape[2] - 2
    stacked = jnp.concatenate(
        [
            padded[
                time_off : time_off + frames,
                row_off : row_off + height,
                col_off : col_off + breadth,
            ]
            for time_off in range(3)
            for row_off in range(3)
            for col_off in range(3)
        ],
        -1,
    )
    kernel = conv_weight.reshape(-1, conv_weight.shape[-1])
    linear = (
        jnp.dot(stacked.reshape(-1, stacked.shape[-1]), kernel, preferred_element_type=jnp.float32)
        + conv_bias
    )
    normed = linear * lax.rsqrt(jnp.mean(linear * linear, -1, keepdims=True) + 1e-06) * norm_gain
    return jax.nn.silu(normed).astype(jnp.bfloat16).reshape(frames, height, breadth, -1)


def attend_block(carried, block_keys, block_values, query_heads):
    running, denominator, weighted = carried
    scores = jnp.einsum("hqd,khd->hqk", query_heads, block_keys, preferred_element_type=jnp.float32)
    scores = scores * query_heads.shape[-1] ** (-0.5)
    newmax = jnp.maximum(running, jnp.max(scores, -1))
    factor = jnp.exp(running - newmax)
    weights = jnp.exp(scores - newmax[..., None])
    denominator = denominator * factor + jnp.sum(weights, -1)
    product = jnp.einsum(
        "hqk,khd->hqd",
        weights.astype(jnp.bfloat16),
        block_values,
        preferred_element_type=jnp.float32,
    )
    weighted = weighted * factor[..., None] + product
    return (newmax, denominator, weighted)


def fold_pieces(query_heads, carried, pieces):
    key_piece, value_piece = pieces
    frames, height, breadth = (key_piece.shape[0], key_piece.shape[1], key_piece.shape[2])
    heads_here, head_width = (query_heads.shape[0], query_heads.shape[2])
    group_rows = 4

    def regroup(one_piece):
        shaped = one_piece.reshape(
            frames, height // group_rows, group_rows, breadth, heads_here, head_width
        )
        shaped = shaped.transpose(1, 0, 2, 3, 4, 5)
        return shaped.reshape(
            height // group_rows, frames * group_rows * breadth, heads_here, head_width
        )

    def advance(inner, blocks):
        return (attend_block(inner, blocks[0], blocks[1], query_heads), None)

    carried, _ = lax.scan(advance, carried, (regroup(key_piece), regroup(value_piece)))
    return carried


def on_device(
    queries,
    attn_keys,
    attn_values,
    residual,
    out_weight,
    out_gate,
    head_shift,
    head_scale,
    head_weight,
    head_bias,
    conv_weight,
    conv_bias,
    norm_gain,
):
    head_count = lax.axis_size("head")
    frames_dev = queries.shape[0]
    group_width = queries.shape[3] // head_count
    head_width = HEAD_DIM
    heads_here = group_width // head_width
    local_queries, local_keys, local_values = (
        lax.all_to_all(queries, "head", split_axis=3, concat_axis=0, tiled=True),
        lax.all_to_all(attn_keys, "head", split_axis=3, concat_axis=0, tiled=True),
        lax.all_to_all(attn_values, "head", split_axis=3, concat_axis=0, tiled=True),
    )
    frames_all, height, breadth = (
        local_queries.shape[0],
        local_queries.shape[1],
        local_queries.shape[2],
    )
    count = frames_all * height * breadth
    query_heads = local_queries.reshape(count, heads_here, head_width).transpose(1, 0, 2)
    initial = (
        jnp.full((heads_here, count), -1e30, jnp.float32),
        jnp.zeros((heads_here, count), jnp.float32),
        jnp.zeros((heads_here, count, head_width), jnp.float32),
    )
    carried = fold_pieces(
        query_heads,
        initial,
        (
            lax.all_gather(local_keys, "seq", axis=1, tiled=True),
            lax.all_gather(local_values, "seq", axis=1, tiled=True),
        ),
    )
    running, denominator, weighted = carried
    attended = (weighted / denominator[..., None]).astype(jnp.bfloat16)
    attended = attended.transpose(1, 0, 2).reshape(count, group_width)
    partial_value = jnp.dot(
        attended,
        lax.all_gather(out_weight, "seq", axis=1, tiled=True),
        preferred_element_type=jnp.float32,
    )
    partial_value = partial_value.reshape(frames_all, height, breadth, partial_value.shape[-1])
    owned = lax.psum_scatter(
        partial_value.astype(jnp.bfloat16), "head", scatter_dimension=0, tiled=True
    ).astype(jnp.float32)
    hidden = (residual.astype(jnp.float32) + out_gate * owned).astype(jnp.bfloat16)
    own_video = head_latent(hidden, head_shift, head_scale, head_weight, head_bias)
    earlier = from_behind(own_video, "head", 1)
    video = jnp.concatenate([earlier, own_video], 0)
    extended = padded_2(video, (("seq", 1),), 1)
    padded = jnp.pad(extended, ((0, 0), (0, 0), (1, 1), (0, 0)))
    features = convolve(padded, frames_dev, conv_weight, conv_bias, norm_gain)
    return (hidden, features)


def solution(mesh):
    return jax.shard_map(
        on_device,
        mesh=mesh,
        in_specs=(
            P(("clip", "head"), "seq", None, None),
            P(("clip", "head"), "seq", None, None),
            P(("clip", "head"), "seq", None, None),
            P(("clip", "head"), "seq", None, None),
            P("head", "seq"),
            P(),
            P(),
            P(),
            P(),
            P(),
            P(),
            P(),
            P(),
        ),
        out_specs=(P(("clip", "head"), "seq", None, None), P(("clip", "head"), "seq", None, None)),
        check_vma=False,
    )
```

profile of v0, /device:TPU:2, one launch (start us, length us, event | category | flops | bytes accessed | tf_op | source)
XLA Modules:
  0.0 232.1 jit_solution(3632974338613475676)
XLA Ops:
  8.2 1.8 copy.79
  10.0 2.3 reshape.122
  12.3 3.4 %all-to-all-start.1 = ((bf16[4,2,12288]{2,1,0:T(2,128)(2,1)}), bf16[4,2,12288]{2,1,0:T(2,128)(2,1)S(1)}, u32[]{:S(2)}, u32[]{:S(2)}) async-start(bf16[4,2,12288]{2,1,0:T(2,128)(2,1)} %reshape.122), calls=%async_computation.1 | async-start | bytes 393216 | tf_op jit(solution)/shard_map/all_to_all | solution.py:132
  15.6 1.8 copy.75
  17.5 2.3 reshape.124
  19.8 4.4 %all-to-all-start = ((bf16[4,2,12288]{2,1,0:T(2,128)(2,1)}), bf16[4,2,12288]{2,1,0:T(2,128)(2,1)S(1)}, u32[]{:S(2)}, u32[]{:S(2)}) async-start(bf16[4,2,12288]{2,1,0:T(2,128)(2,1)} %reshape.124), calls=%async_computation | async-start | bytes 393216 | tf_op jit(solution)/shard_map/all_to_all | solution.py:131
  24.2 1.8 copy.84
  26.0 2.3 reshape.126
  30.6 4.0 %all-to-all-start.2 = ((bf16[4,2,12288]{2,1,0:T(2,128)(2,1)}), bf16[4,2,12288]{2,1,0:T(2,128)(2,1)}, u32[]{:S(2)}, u32[]{:S(2)}) async-start(bf16[4,2,12288]{2,1,0:T(2,128)(2,1)} %reshape.126), calls=%async_computation.2 | async-start | bytes 393216 | tf_op jit(solution)/shard_map/all_to_all | solution.py:133
  34.7 35.2 %all_gather.9 = bf16[8,4,16,768]{3,2,0,1:T(8,128)(2,1)S(1)} all-gather(bf16[8,1,16,768]{3,2,0,1:T(8,128)(2,1)S(1)} %bitcast.111), channel_id=1, replica_groups=mesh['clip'=2,'seq'=4,'head'=4] {'seq'}, dimensions={1}, use_global_device_ids=true | all-gather | bytes 983040 | tf_op jit(solution)/shard_map/all_gather | solution.py:151
  70.8 1.2 reshape.125
  73.4 5.6 %reshape.127 = bf16[3072,1,2,16]{3,2,1,0:T(2,128)(2,1)S(1)} reshape(bf16[4,2,12288]{2,1,0:T(2,128)(2,1)} %all-to-all-done.2) | data formatting | bytes 393216
  79.0 2.5 %copy.94 = bf16[2,1,16,4,768]{4,3,2,0,1:T(4,128)(2,1)} copy(bf16[2,1,16,4,768]{2,0,4,3,1:T(2,128)(2,1)S(1)} %bitcast.95) | data formatting | bytes 393216 | tf_op jit(solution)/shard_map/all_to_all | solution.py:133
  82.4 32.4 %all_gather.10 = bf16[8,4,16,768]{3,2,0,1:T(8,128)(2,1)S(1)} all-gather(bf16[8,1,16,768]{3,2,0,1:T(8,128)(2,1)S(1)} %bitcast.112), channel_id=1, replica_groups=mesh['clip'=2,'seq'=4,'head'=4] {'seq'}, dimensions={1}, use_global_device_ids=true | all-gather | bytes 983040 | tf_op jit(solution)/shard_map/all_gather | solution.py:152
  114.9 1.9 squeeze.10
  119.1 57.9 %all-gather.2.cloned.1.call-done = bf16[768,5120]{1,0:T(8,128)(2,1)} async-done(((bf16[768,1280]{1,0:T(8,128)(2,1)}), bf16[768,5120]{1,0:T(8,128)(2,1)}) %all-gather.2.cloned.1.call-update) | async-done | bytes 7864336 | tf_op jit(solution)/shard_map/all_gather | solution.py:160
  177.0 5.6 %fusion.5 = bf16[8,1,16,5120]{3,2,0,1:T(8,128)(2,1)} fusion(bf16[8,16,768]{2,1,0:T(8,128)(2,1)S(1)} %dot_general.24, bf16[768,5120]{1,0:T(8,128)(2,1)} %all-gather.2.cloned.1.call-done), kind=kOutput, calls=%fused_computation.3 | convolution fusion | flops 1007288320 | bytes 9371648 | tf_op jit(solution)/shard_map/dot_general | solution.py:158
  182.6 23.7 %reduce-scatter.2.cloned.1.call-done = bf16[2,1,16,5120]{3,2,0,1:T(8,128)(2,1)} async-done(((bf16[8,1,16,5120]{3,2,0,1:T(8,128)(2,1)}), bf16[2,1,16,5120]{3,2,0,1:T(8,128)(2,1)}) %reduce-scatter.2.cloned.1.call-update) | async-done | bytes 327696 | tf_op jit(solution)/shard_map/reduce_scatter | solution.py:164
  206.3 1.2 convert_reduce_fusion
  208.4 1.9 collective-permute-start
  210.4 3.3 %collective-permute-done = bf16[2,2,32,16]{3,2,1,0:T(8,128)(2,1)S(1)} collective-permute-done((bf16[2,2,32,16]{3,2,1,0:T(8,128)(2,1)S(1)}, bf16[2,2,32,16]{3,2,1,0:T(8,128)(2,1)S(1)}, u32[]{:S(2)}, u32[]{:S(2)}) %collective-permute-start) | collective-permute-done | bytes 4128 | tf_op jit(solution)/shard_map/ppermute | solution.py:12
  213.7 3.6 %collective-permute-start.1 = (bf16[4,1,32,16]{3,2,1,0:T(8,128)(2,1)S(1)}, bf16[4,1,32,16]{3,2,1,0:T(8,128)(2,1)S(1)}, u32[]{:S(2)}, u32[]{:S(2)}) collective-permute-start(bf16[4,1,32,16]{3,2,1,0:T(8,128)(2,1)S(1)} %get-tuple-element.63), channel_id=1, source_target_pairs={{0,4},{4,8},{8,12},{1,5},{5,9},{9,13},{2,6},{6,10},{10,14},{3,7},{... | collective-permute-start | bytes 12296 | tf_op jit(solution)/shard_map/ppermute | solution.py:22
  217.3 1.3 collective-permute-start.2
  218.9 4.2 %collective-permute-done.2 = bf16[4,1,32,16]{3,2,1,0:T(8,128)(2,1)S(1)} collective-permute-done((bf16[4,1,32,16]{3,2,1,0:T(8,128)(2,1)S(1)}, bf16[4,1,32,16]{3,2,1,0:T(8,128)(2,1)S(1)}, u32[]{:S(2)}, u32[]{:S(2)}) %collective-permute-start.2) | collective-permute-done | bytes 4128 | tf_op jit(solution)/shard_map/ppermute | solution.py:23
  (71 shorter events, 12.1 us)
Async XLA Ops:
  7.2 200.8 %copy-start = (bf16[5120,64]{0,1:T(8,128)(2,1)S(1)}, bf16[5120,64]{0,1:T(8,128)(2,1)}, u32[]{:S(2)}) copy-start(bf16[5120,64]{0,1:T(8,128)(2,1)} %param.21) | copy-start | bytes 1966084
  7.2 1.0 copy-start.5
  7.2 169.8 %all-gather.2.cloned.1.call-start = ((), (), s32[]{:S(2)}) async-start(), calls=%async_computation.4 | async-start | bytes 9830400 | tf_op jit(solution)/shard_map/all_gather | solution.py:160
  8.2 7.4 %copy-start.6 = (bf16[2,1,16,3072]{3,2,1,0:T(8,128)(2,1)S(1)}, bf16[2,1,16,3072]{3,2,1,0:T(8,128)(2,1)}, u32[]{:S(2)}) copy-start(bf16[2,1,16,3072]{3,2,1,0:T(8,128)(2,1)} %param.13) | copy-start | bytes 589828
  12.3 7.5 %all-to-all-start.1 = ((bf16[4,2,12288]{2,1,0:T(2,128)(2,1)}), bf16[4,2,12288]{2,1,0:T(2,128)(2,1)S(1)}, u32[]{:S(2)}, u32[]{:S(2)}) async-start(bf16[4,2,12288]{2,1,0:T(2,128)(2,1)} %reshape.122), calls=%async_computation.1 | async-start | bytes 393216 | tf_op jit(solution)/shard_map/all_to_all | solution.py:132
  17.5 6.7 %copy-start.7 = (bf16[2,1,16,3072]{3,2,1,0:T(8,128)(2,1)S(1)}, bf16[2,1,16,3072]{3,2,1,0:T(8,128)(2,1)}, u32[]{:S(2)}) copy-start(bf16[2,1,16,3072]{3,2,1,0:T(8,128)(2,1)} %param.15) | copy-start | bytes 589828
  19.8 10.8 %all-to-all-start = ((bf16[4,2,12288]{2,1,0:T(2,128)(2,1)}), bf16[4,2,12288]{2,1,0:T(2,128)(2,1)S(1)}, u32[]{:S(2)}, u32[]{:S(2)}) async-start(bf16[4,2,12288]{2,1,0:T(2,128)(2,1)} %reshape.124), calls=%async_computation | async-start | bytes 393216 | tf_op jit(solution)/shard_map/all_to_all | solution.py:131
  30.6 42.8 %all-to-all-start.2 = ((bf16[4,2,12288]{2,1,0:T(2,128)(2,1)}), bf16[4,2,12288]{2,1,0:T(2,128)(2,1)}, u32[]{:S(2)}, u32[]{:S(2)}) async-start(bf16[4,2,12288]{2,1,0:T(2,128)(2,1)} %reshape.126), calls=%async_computation.2 | async-start | bytes 393216 | tf_op jit(solution)/shard_map/all_to_all | solution.py:133
  34.6 171.7 %reduce-scatter.2.cloned.1.call-start = ((), (), s32[]{:S(2)}) async-start(), calls=%async_computation.5 | async-start | bytes 1638400 | tf_op jit(solution)/shard_map/reduce_scatter | solution.py:164
  116.8 1.2 copy-start.2
  119.1 63.5 %copy-start.9 = (f32[5120]{0:T(1024)S(1)}, f32[5120]{0:T(1024)}, u32[]{:S(2)}) copy-start(f32[5120]{0:T(1024)} %param.20) | copy-start | bytes 61444
  119.1 87.2 %copy-start.10 = (f32[5120]{0:T(1024)S(1)}, f32[5120]{0:T(1024)}, u32[]{:S(2)}) copy-start(f32[5120]{0:T(1024)} %param.18) | copy-start | bytes 61444
  182.6 23.8 %copy-start.4 = (bf16[2,1,16,5120]{3,2,1,0:T(8,128)(2,1)S(1)}, bf16[2,1,16,5120]{3,2,1,0:T(8,128)(2,1)}, u32[]{:S(2)}) copy-start(bf16[2,1,16,5120]{3,2,1,0:T(8,128)(2,1)} %param.16) | copy-start | bytes 983044
  182.6 25.2 %copy-start.8 = (f32[5120]{0:T(1024)S(1)}, f32[5120]{0:T(1024)}, u32[]{:S(2)}) copy-start(f32[5120]{0:T(1024)} %param.19) | copy-start | bytes 61444
  182.6 25.4 %copy-start.13 = (f32[64]{0:T(128)S(1)}, f32[64]{0:T(128)}, u32[]{:S(2)}) copy-start(f32[64]{0:T(128)} %param.22) | copy-start | bytes 772
  207.5 15.8 %copy-start.1 = (bf16[2,1,16,5120]{3,2,0,1:T(8,128)(2,1)}, bf16[2,1,16,5120]{3,2,0,1:T(8,128)(2,1)S(1)}, u32[]{:S(2)}) copy-start(bf16[2,1,16,5120]{3,2,0,1:T(8,128)(2,1)S(1)} %get-tuple-element.36) | copy-start | bytes 983044
  208.4 5.2 %collective-permute-start = (bf16[2,2,32,16]{3,2,1,0:T(8,128)(2,1)S(1)}, bf16[2,2,32,16]{3,2,1,0:T(8,128)(2,1)S(1)}, u32[]{:S(2)}, u32[]{:S(2)}) collective-permute-start(bf16[2,2,32,16]{3,2,1,0:T(8,128)(2,1)S(1)} %bitcast.101), channel_id=1, source_target_pairs={{0,1},{1,2},{2,3},{4,5},{5,6},{6,7},{8,9},{9,10},{10,11},{12,13},{... | collective-permute-start | bytes 12296 | tf_op jit(solution)/shard_map/ppermute | solution.py:12
  213.7 5.2 %collective-permute-start.1 = (bf16[4,1,32,16]{3,2,1,0:T(8,128)(2,1)S(1)}, bf16[4,1,32,16]{3,2,1,0:T(8,128)(2,1)S(1)}, u32[]{:S(2)}, u32[]{:S(2)}) collective-permute-start(bf16[4,1,32,16]{3,2,1,0:T(8,128)(2,1)S(1)} %get-tuple-element.63), channel_id=1, source_target_pairs={{0,4},{4,8},{8,12},{1,5},{5,9},{9,13},{2,6},{6,10},{10,14},{3,7},{... | collective-permute-start | bytes 12296 | tf_op jit(solution)/shard_map/ppermute | solution.py:22
  217.3 5.8 %collective-permute-start.2 = (bf16[4,1,32,16]{3,2,1,0:T(8,128)(2,1)S(1)}, bf16[4,1,32,16]{3,2,1,0:T(8,128)(2,1)S(1)}, u32[]{:S(2)}, u32[]{:S(2)}) collective-permute-start(bf16[4,1,32,16]{3,2,1,0:T(8,128)(2,1)S(1)} %get-tuple-element.64), channel_id=1, source_target_pairs={{4,0},{8,4},{12,8},{5,1},{9,5},{13,9},{6,2},{10,6},{14,10},{7,3},{... | collective-permute-start | bytes 12296 | tf_op jit(solution)/shard_map/ppermute | solution.py:23
  223.2 1.0 copy-start.3
  223.2 1.0 copy-start.11
  223.2 1.3 copy-start.12
Sparse Core Ops, SparseCore 0:
  9.6 167.3 all-gather.1
  182.7 23.5 reduce-scatter.1
where the time goes:
time: 233 us; the launch traced here: 232 us
  waiting for transfers between devices  90.1 us (39%)
  blocking collectives  67.6 us (29%)
  local copies, waits for them, and re-layouts  30.9 us (13%)
  starting transfers between devices  18.7 us (8%)
  between operations  14.4 us (6%)
  matrix products  7.28 us (3%)
  other arithmetic  3.08 us (1%)
    all_gather x1, waiting for transfers between devices, on_device(): lax.all_gather(out_weight, 'seq', axis=1, tiled=True)  57.9 us
    all_gather x1, blocking collectives, on_device(): lax.all_gather(local_keys, 'seq', axis=1, tiled=True)  35.2 us
    all_gather x1, blocking collectives, on_device(): lax.all_gather(local_values, 'seq', axis=1, tiled=True)  32.4 us
    reduce_scatter x1, waiting for transfers between devices, on_device(): lax.psum_scatter(partial_value.astype(jnp.bfloat16), 'head', scatter_dime...  23.7 us
    unnamed x37, local copies, waits for them, and re-layouts  21.1 us
    dot_general x1, matrix products, on_device(): jnp.dot(attended, lax.all_gather(out_weight, 'seq', axis=1, tiled=True),...  5.58 us
  transfers between devices with their start and end apart: 8, of which 5 were waited for; matrix products, arithmetic and copies ran while one was open for 13% of the time, Pallas kernels for 0%

commit v1 on v0

--- a/solution.py
+++ b/solution.py
@@ -4,6 +4,17 @@
 from jax.sharding import PartitionSpec as P
 
 HEAD_DIM = 128
+
+
+def ring_gather(value, axis, dim):
+    ways = lax.axis_size(axis)
+    pieces = [value]
+    for far in range(1, ways):
+        pieces.append(
+            lax.ppermute(pieces[far - 1], axis, [(d, (d - 1) % ways) for d in range(ways)])
+        )
+    line = jnp.concatenate(pieces, axis=dim)
+    return jnp.roll(line, lax.axis_index(axis) * value.shape[dim], axis=dim)
 
 
 def from_behind(value, axis, steps):
@@ -148,7 +159,7 @@
         query_heads,
         initial,
         (
-            lax.all_gather(local_keys, "seq", axis=1, tiled=True),
+            ring_gather(local_keys, "seq", 1),
             lax.all_gather(local_values, "seq", axis=1, tiled=True),
         ),
     )

time: 233 us -> 233 us (level)
  waiting for transfers between devices: 90.1 us -> 108 us
  blocking collectives: 67.6 us -> 51.1 us
  local copies, waits for them, and re-layouts: 30.9 us -> 27.7 us
    all_gather x1 -> x0, blocking collectives: 35.2 us -> none  [on_device(): lax.all_gather(local_keys, 'seq', axis=1, tiled=True)]
    ppermute x0 -> x3, waiting for transfers between devices: none -> 13.6 us  [ring_gather(): lax.ppermute(pieces[far - 1], axis, [(d, (d - 1) % ways) for d in range(w...]
    all_gather x1, blocking collectives: 32.4 us -> 44.4 us  [on_device(): lax.all_gather(local_values, 'seq', axis=1, tiled=True)]
    all_to_all x0 -> x1, blocking collectives: none -> 6.76 us  [on_device(): lax.all_to_all(attn_keys, 'head', split_axis=3, concat_axis=0, tiled=True)]
    ppermute x0 -> x3, starting transfers between devices: none -> 4.39 us  [ring_gather(): lax.ppermute(pieces[far - 1], axis, [(d, (d - 1) % ways) for d in range(w...]
    all_gather x1, waiting for transfers between devices: 57.9 us -> 61.4 us  [on_device(): lax.all_gather(out_weight, 'seq', axis=1, tiled=True)]
    all_to_all x1 -> x0, starting transfers between devices: 3.36 us -> none  [on_device(): lax.all_to_all(attn_keys, 'head', split_axis=3, concat_axis=0, tiled=True)]
    all_to_all x2, local copies, waits for them, and re-layouts: 3.47 us -> 1.11 us  [on_device(): lax.all_to_all(attn_values, 'head', split_axis=3, concat_axis=0, tiled=True)]
  transfers between devices with their start and end apart: 8 -> 10, of which waited for: 5 -> 6; matrix products, arithmetic and copies ran while one was open for 13% -> 12% of each run, Pallas kernels for 0% -> 0%
where the time goes in v1:
time: 233 us; the launch traced here: 232 us
  waiting for transfers between devices  108 us (46%)
  blocking collectives  51.1 us (22%)
  local copies, waits for them, and re-layouts  27.7 us (12%)
  starting transfers between devices  20.7 us (9%)
  between operations  14.5 us (6%)
  matrix products  7.22 us (3%)
  other arithmetic  2.78 us (1%)
    all_gather x1, waiting for transfers between devices, on_device(): lax.all_gather(out_weight, 'seq', axis=1, tiled=True)  61.4 us
    all_gather x1, blocking collectives, on_device(): lax.all_gather(local_values, 'seq', axis=1, tiled=True)  44.4 us
    reduce_scatter x1, waiting for transfers between devices, on_device(): lax.psum_scatter(partial_value.astype(jnp.bfloat16), 'head', scatter_dime...  24.5 us
    unnamed x44, local copies, waits for them, and re-layouts  20.2 us
    ppermute x3, waiting for transfers between devices, ring_gather(): lax.ppermute(pieces[far - 1], axis, [(d, (d - 1) % ways) for d in range(w...  13.6 us
    all_to_all x1, blocking collectives, on_device(): lax.all_to_all(attn_keys, 'head', split_axis=3, concat_axis=0, tiled=True)  6.76 us
    dot_general x1, matrix products, on_device(): jnp.dot(attended, lax.all_gather(out_weight, 'seq', axis=1, tiled=True),...  5.58 us
    all_to_all x1, starting transfers between devices, on_device(): lax.all_to_all(attn_values, 'head', split_axis=3, concat_axis=0, tiled=True)  4.97 us
  transfers between devices with their start and end apart: 10, of which 6 were waited for; matrix products, arithmetic and copies ran while one was open for 12% of the time, Pallas kernels for 0%

profile of v1, /device:TPU:2, one launch (start us, length us, event | category | flops | bytes accessed | tf_op | source)
XLA Modules:
  0.0 232.0 jit_solution(13914991369603621615)
XLA Ops:
  8.2 1.8 copy.80
  10.0 1.6 reshape.122
  11.6 6.8 %all_to_all.51 = bf16[4,2,12288]{2,1,0:T(2,128)(2,1)S(1)} all-to-all(bf16[4,2,12288]{2,1,0:T(2,128)(2,1)S(1)} %reshape.122), channel_id=1, replica_groups=mesh['clip'=2,'seq'=4,'head'=4] {'head'}, dimensions={0} | all-to-all | bytes 393216 | tf_op jit(solution)/shard_map/all_to_all | solution.py:143
  18.3 1.2 reshape.123
  20.6 3.7 %collective-permute-start = (bf16[8,1,16,768]{3,2,0,1:T(8,128)(2,1)S(1)}, bf16[8,1,16,768]{3,2,0,1:T(8,128)(2,1)}, u32[]{:S(2)}, u32[]{:S(2)}) collective-permute-start(bf16[8,1,16,768]{3,2,0,1:T(8,128)(2,1)S(1)} %bitcast.110), channel_id=1, source_target_pairs={{0,12},{4,0},{8,4},{12,8},{1,13},{5,1},{9,5},{13,9},{2,14},{6,2},{... | collective-permute-start | bytes 589832 | tf_op jit(solution)/shard_map/ppermute | solution.py:14
  24.3 1.8 copy.89
  26.1 2.3 reshape.126
  28.4 5.0 %all-to-all-start.2 = ((bf16[4,2,12288]{2,1,0:T(2,128)(2,1)}), bf16[4,2,12288]{2,1,0:T(2,128)(2,1)S(1)}, u32[]{:S(2)}, u32[]{:S(2)}) async-start(bf16[4,2,12288]{2,1,0:T(2,128)(2,1)} %reshape.126), calls=%async_computation.2 | async-start | bytes 393216 | tf_op jit(solution)/shard_map/all_to_all | solution.py:144
  33.4 1.8 copy.84
  35.2 2.3 reshape.124
  37.5 4.6 %all-to-all-start.1 = ((bf16[4,2,12288]{2,1,0:T(2,128)(2,1)}), bf16[4,2,12288]{2,1,0:T(2,128)(2,1)S(1)}, u32[]{:S(2)}, u32[]{:S(2)}) async-start(bf16[4,2,12288]{2,1,0:T(2,128)(2,1)} %reshape.124), calls=%async_computation.1 | async-start | bytes 393216 | tf_op jit(solution)/shard_map/all_to_all | solution.py:142
  44.8 44.4 %all_gather.6 = bf16[8,4,16,768]{3,2,0,1:T(8,128)(2,1)S(1)} all-gather(bf16[8,1,16,768]{3,2,0,1:T(8,128)(2,1)S(1)} %bitcast.124), channel_id=1, replica_groups=mesh['clip'=2,'seq'=4,'head'=4] {'seq'}, dimensions={1}, use_global_device_ids=true | all-gather | bytes 983040 | tf_op jit(solution)/shard_map/all_gather | solution.py:163
  89.2 1.2 reshape.125
  91.8 1.9 squeeze.10
  95.9 13.6 %collective-permute-done.2 = bf16[8,1,16,768]{3,2,0,1:T(8,128)(2,1)S(1)} collective-permute-done((bf16[8,1,16,768]{3,2,0,1:T(8,128)(2,1)}, bf16[8,1,16,768]{3,2,0,1:T(8,128)(2,1)S(1)}, u32[]{:S(2)}, u32[]{:S(2)}) %collective-permute-start.2) | collective-permute-done | bytes 196640 | tf_op jit(solution)/shard_map/ppermute | solution.py:14
  114.8 61.4 %all-gather.2.cloned.1.call-done = bf16[768,5120]{1,0:T(8,128)(2,1)} async-done(((bf16[768,1280]{1,0:T(8,128)(2,1)}), bf16[768,5120]{1,0:T(8,128)(2,1)}) %all-gather.2.cloned.1.call-update) | async-done | bytes 7864336 | tf_op jit(solution)/shard_map/all_gather | solution.py:171
  176.2 5.6 %fusion.5 = bf16[8,1,16,5120]{3,2,0,1:T(8,128)(2,1)} fusion(bf16[8,16,768]{2,1,0:T(8,128)(2,1)S(1)} %dot_general.24, bf16[768,5120]{1,0:T(8,128)(2,1)} %all-gather.2.cloned.1.call-done), kind=kOutput, calls=%fused_computation.3 | convolution fusion | flops 1007288320 | bytes 9371648 | tf_op jit(solution)/shard_map/dot_general | solution.py:169
  181.8 24.5 %reduce-scatter.2.cloned.1.call-done = bf16[2,1,16,5120]{3,2,0,1:T(8,128)(2,1)} async-done(((bf16[8,1,16,5120]{3,2,0,1:T(8,128)(2,1)}), bf16[2,1,16,5120]{3,2,0,1:T(8,128)(2,1)}) %reduce-scatter.2.cloned.1.call-update) | async-done | bytes 327696 | tf_op jit(solution)/shard_map/reduce_scatter | solution.py:175
  206.3 1.2 convert_reduce_fusion
  208.4 1.9 collective-permute-start.3
  210.3 3.3 %collective-permute-done.3 = bf16[2,2,32,16]{3,2,1,0:T(8,128)(2,1)S(1)} collective-permute-done((bf16[2,2,32,16]{3,2,1,0:T(8,128)(2,1)S(1)}, bf16[2,2,32,16]{3,2,1,0:T(8,128)(2,1)S(1)}, u32[]{:S(2)}, u32[]{:S(2)}) %collective-permute-start.3) | collective-permute-done | bytes 4128 | tf_op jit(solution)/shard_map/ppermute | solution.py:23
  213.6 3.6 %collective-permute-start.4 = (bf16[4,1,32,16]{3,2,1,0:T(8,128)(2,1)S(1)}, bf16[4,1,32,16]{3,2,1,0:T(8,128)(2,1)S(1)}, u32[]{:S(2)}, u32[]{:S(2)}) collective-permute-start(bf16[4,1,32,16]{3,2,1,0:T(8,128)(2,1)S(1)} %get-tuple-element.63), channel_id=1, source_target_pairs={{0,4},{4,8},{8,12},{1,5},{5,9},{9,13},{2,6},{6,10},{10,14},{3,7},{... | collective-permute-start | bytes 12296 | tf_op jit(solution)/shard_map/ppermute | solution.py:33
  217.2 1.3 collective-permute-start.5
  218.8 4.2 %collective-permute-done.5 = bf16[4,1,32,16]{3,2,1,0:T(8,128)(2,1)S(1)} collective-permute-done((bf16[4,1,32,16]{3,2,1,0:T(8,128)(2,1)S(1)}, bf16[4,1,32,16]{3,2,1,0:T(8,128)(2,1)S(1)}, u32[]{:S(2)}, u32[]{:S(2)}) %collective-permute-start.5) | collective-permute-done | bytes 4128 | tf_op jit(solution)/shard_map/ppermute | solution.py:34
  (84 shorter events, 16.9 us)
Async XLA Ops:
  7.2 200.8 %copy-start = (bf16[5120,64]{0,1:T(8,128)(2,1)S(1)}, bf16[5120,64]{0,1:T(8,128)(2,1)}, u32[]{:S(2)}) copy-start(bf16[5120,64]{0,1:T(8,128)(2,1)} %param.21) | copy-start | bytes 1966084
  7.2 1.0 copy-start.5
  7.2 169.0 %all-gather.2.cloned.1.call-start = ((), (), s32[]{:S(2)}) async-start(), calls=%async_computation.4 | async-start | bytes 9830400 | tf_op jit(solution)/shard_map/all_gather | solution.py:171
  18.3 6.0 %copy-start.6 = (bf16[2,1,16,3072]{3,2,1,0:T(8,128)(2,1)S(1)}, bf16[2,1,16,3072]{3,2,1,0:T(8,128)(2,1)}, u32[]{:S(2)}) copy-start(bf16[2,1,16,3072]{3,2,1,0:T(8,128)(2,1)} %param.15) | copy-start | bytes 589828
  20.6 12.7 %copy-start.7 = (bf16[2,1,16,3072]{3,2,1,0:T(8,128)(2,1)S(1)}, bf16[2,1,16,3072]{3,2,1,0:T(8,128)(2,1)}, u32[]{:S(2)}) copy-start(bf16[2,1,16,3072]{3,2,1,0:T(8,128)(2,1)} %param.13) | copy-start | bytes 589828
  20.6 23.7 %collective-permute-start = (bf16[8,1,16,768]{3,2,0,1:T(8,128)(2,1)S(1)}, bf16[8,1,16,768]{3,2,0,1:T(8,128)(2,1)}, u32[]{:S(2)}, u32[]{:S(2)}) collective-permute-start(bf16[8,1,16,768]{3,2,0,1:T(8,128)(2,1)S(1)} %bitcast.110), channel_id=1, source_target_pairs={{0,12},{4,0},{8,4},{12,8},{1,13},{5,1},{9,5},{13,9},{2,14},{6,2},{... | collective-permute-start | bytes 589832 | tf_op jit(solution)/shard_map/ppermute | solution.py:14
  28.4 9.1 %all-to-all-start.2 = ((bf16[4,2,12288]{2,1,0:T(2,128)(2,1)}), bf16[4,2,12288]{2,1,0:T(2,128)(2,1)S(1)}, u32[]{:S(2)}, u32[]{:S(2)}) async-start(bf16[4,2,12288]{2,1,0:T(2,128)(2,1)} %reshape.126), calls=%async_computation.2 | async-start | bytes 393216 | tf_op jit(solution)/shard_map/all_to_all | solution.py:144
  37.5 51.7 %all-to-all-start.1 = ((bf16[4,2,12288]{2,1,0:T(2,128)(2,1)}), bf16[4,2,12288]{2,1,0:T(2,128)(2,1)S(1)}, u32[]{:S(2)}, u32[]{:S(2)}) async-start(bf16[4,2,12288]{2,1,0:T(2,128)(2,1)} %reshape.124), calls=%async_computation.1 | async-start | bytes 393216 | tf_op jit(solution)/shard_map/all_to_all | solution.py:142
  42.0 164.3 %reduce-scatter.2.cloned.1.call-start = ((), (), s32[]{:S(2)}) async-start(), calls=%async_computation.5 | async-start | bytes 1638400 | tf_op jit(solution)/shard_map/reduce_scatter | solution.py:175
  44.3 49.4 %collective-permute-start.1 = (bf16[8,1,16,768]{3,2,0,1:T(8,128)(2,1)}, bf16[8,1,16,768]{3,2,0,1:T(8,128)(2,1)}, u32[]{:S(2)}, u32[]{:S(2)}) collective-permute-start(bf16[8,1,16,768]{3,2,0,1:T(8,128)(2,1)} %collective-permute-done), channel_id=1, source_target_pairs={{0,12},{4,0},{8,4},{12,8},{1,13},{5,1},{9,5},{13,9},{2,14},{6,2},{... | collective-permute-start | bytes 589832 | tf_op jit(solution)/shard_map/ppermute | solution.py:14
  93.8 15.7 %collective-permute-start.2 = (bf16[8,1,16,768]{3,2,0,1:T(8,128)(2,1)}, bf16[8,1,16,768]{3,2,0,1:T(8,128)(2,1)S(1)}, u32[]{:S(2)}, u32[]{:S(2)}) collective-permute-start(bf16[8,1,16,768]{3,2,0,1:T(8,128)(2,1)} %collective-permute-done.1), channel_id=1, source_target_pairs={{0,12},{4,0},{8,4},{12,8},{1,13},{5,1},{9,5},{13,9},{2,14},{6,2},{... | collective-permute-start | bytes 589832 | tf_op jit(solution)/shard_map/ppermute | solution.py:14
  112.4 1.2 copy-start.2
  114.7 67.1 %copy-start.9 = (f32[5120]{0:T(1024)S(1)}, f32[5120]{0:T(1024)}, u32[]{:S(2)}) copy-start(f32[5120]{0:T(1024)} %param.20) | copy-start | bytes 61444
  114.8 91.5 %copy-start.10 = (f32[5120]{0:T(1024)S(1)}, f32[5120]{0:T(1024)}, u32[]{:S(2)}) copy-start(f32[5120]{0:T(1024)} %param.18) | copy-start | bytes 61444
  181.8 24.5 %copy-start.4 = (bf16[2,1,16,5120]{3,2,1,0:T(8,128)(2,1)S(1)}, bf16[2,1,16,5120]{3,2,1,0:T(8,128)(2,1)}, u32[]{:S(2)}) copy-start(bf16[2,1,16,5120]{3,2,1,0:T(8,128)(2,1)} %param.16) | copy-start | bytes 983044
  181.8 26.0 %copy-start.8 = (f32[5120]{0:T(1024)S(1)}, f32[5120]{0:T(1024)}, u32[]{:S(2)}) copy-start(f32[5120]{0:T(1024)} %param.19) | copy-start | bytes 61444
  181.8 26.2 %copy-start.13 = (f32[64]{0:T(128)S(1)}, f32[64]{0:T(128)}, u32[]{:S(2)}) copy-start(f32[64]{0:T(128)} %param.22) | copy-start | bytes 772
  207.5 15.8 %copy-start.1 = (bf16[2,1,16,5120]{3,2,0,1:T(8,128)(2,1)}, bf16[2,1,16,5120]{3,2,0,1:T(8,128)(2,1)S(1)}, u32[]{:S(2)}) copy-start(bf16[2,1,16,5120]{3,2,0,1:T(8,128)(2,1)S(1)} %get-tuple-element.36) | copy-start | bytes 983044
  208.4 5.2 %collective-permute-start.3 = (bf16[2,2,32,16]{3,2,1,0:T(8,128)(2,1)S(1)}, bf16[2,2,32,16]{3,2,1,0:T(8,128)(2,1)S(1)}, u32[]{:S(2)}, u32[]{:S(2)}) collective-permute-start(bf16[2,2,32,16]{3,2,1,0:T(8,128)(2,1)S(1)} %bitcast.114), channel_id=1, source_target_pairs={{0,1},{1,2},{2,3},{4,5},{5,6},{6,7},{8,9},{9,10},{10,11},{12,13},{... | collective-permute-start | bytes 12296 | tf_op jit(solution)/shard_map/ppermute | solution.py:23
  213.6 5.2 %collective-permute-start.4 = (bf16[4,1,32,16]{3,2,1,0:T(8,128)(2,1)S(1)}, bf16[4,1,32,16]{3,2,1,0:T(8,128)(2,1)S(1)}, u32[]{:S(2)}, u32[]{:S(2)}) collective-permute-start(bf16[4,1,32,16]{3,2,1,0:T(8,128)(2,1)S(1)} %get-tuple-element.63), channel_id=1, source_target_pairs={{0,4},{4,8},{8,12},{1,5},{5,9},{9,13},{2,6},{6,10},{10,14},{3,7},{... | collective-permute-start | bytes 12296 | tf_op jit(solution)/shard_map/ppermute | solution.py:33
  217.2 5.8 %collective-permute-start.5 = (bf16[4,1,32,16]{3,2,1,0:T(8,128)(2,1)S(1)}, bf16[4,1,32,16]{3,2,1,0:T(8,128)(2,1)S(1)}, u32[]{:S(2)}, u32[]{:S(2)}) collective-permute-start(bf16[4,1,32,16]{3,2,1,0:T(8,128)(2,1)S(1)} %get-tuple-element.64), channel_id=1, source_target_pairs={{4,0},{8,4},{12,8},{5,1},{9,5},{13,9},{6,2},{10,6},{14,10},{7,3},{... | collective-permute-start | bytes 12296 | tf_op jit(solution)/shard_map/ppermute | solution.py:34
  223.1 1.0 copy-start.3
  223.1 1.0 copy-start.11
  223.1 1.3 copy-start.12
Sparse Core Ops, SparseCore 0:
  9.6 166.5 all-gather.1
  181.9 24.3 reduce-scatter.1
